TPU v7x, 256 devices: a whole 4x4x8 slice. The times are simulated.
256 devices in a mesh: rep: 4 (over y), row: 4 (over z_hi), col: 16 (over z_lo, x, core).
Axes of the slice: x: 4, y: 4, z: 8 (z_hi: 4, z_lo: 2; z = z_hi * 2 + z_lo), core: 2. Of those that a mesh axis runs over, the one named last changes fastest.
Arguments:
- patches: bfloat16 [4096, 588], P(('rep', 'col')), may hold values from -20 to 20
- embed_weight: bfloat16 [588, 6144], P(None, 'row'), may hold values from -1 to 1
- embed_bias: float32 [6144], P('row'), may hold values from -3 to 3
- old_in: bfloat16 [64, 768, 1536], P(('row', 'col')), may hold values from -0.078125 to 0.078125
- old_out: bfloat16 [64, 1536, 768], P(('row', 'col')), may hold values from -0.0546875 to 0.0546875
- restore_id: int32 [1], replicated, may hold values from 0 to 47
- norm_gains: float32 [48, 6144], P(None, 'row'), may hold values from 0.1 to 1.9
- in_biases: float32 [48, 12288], P(None, 'col'), may hold values from -3 to 3
- out_biases: float32 [48, 6144], P(None, 'row'), may hold values from -3 to 3
- final_gain: float32 [6144], P('row'), may hold values from 0.1 to 1.9
- check_weight: bfloat16 [6144, 128], P('row'), may hold values from -0.078125 to 0.078125
Outputs:
- in_weight: bfloat16 [6144, 12288], P('row', 'col')
- out_weight: bfloat16 [12288, 6144], P('col', 'row')
- check_logits: float32 [4096, 128], P(('rep', 'col'))
All inputs are finite; a program needn't handle non-finite values.
Results may differ from a plain program's by a relative error of at most 0.0062.
Values may be sent and summed in bfloat16 or wider, within the bound.
A program may use at most 64 MiB of HBM per device.

v0:
```python
import jax
import jax.numpy as jnp
from jax import lax
from jax.sharding import PartitionSpec as P

EPSILON = 1e-06


def from_everyone(shard, axis):
    size = lax.axis_size(axis)
    return lax.all_to_all(
        jnp.broadcast_to(shard[None], (size, *shard.shape)), axis, 0, 0, tiled=True
    )


def taken_together(shard, axis):
    return from_everyone(shard, axis).sum(axis=0)


def packed_total(arrays, axis):
    ends = [0]
    for a in arrays:
        ends.append(ends[-1] + a.size)
    so_far = taken_together(jnp.concatenate([a.ravel() for a in arrays]), axis)
    return tuple((so_far[b:e].reshape(a.shape) for a, b, e in zip(arrays, ends, ends[1:])))


def for_sending(shard):
    return jax.tree.map(lambda a: a.astype(jnp.bfloat16) if a.dtype == jnp.float32 else a, shard)


def partner(value, axis, bit):
    mask = 2**bit
    pairs = [(source, source ^ mask) for source in range(lax.axis_size(axis))]
    return lax.ppermute(value, axis, pairs)


def rows_first(arrays, axis, dims):
    turned = [jnp.moveaxis(a, dim, 0) for a, dim in zip(arrays, dims)]
    widths = [t[0].size for t in turned]
    both = jnp.concatenate([t.reshape(-1, w) for t, w in zip(turned, widths)], axis=1)
    out = lax.all_gather(both, axis, axis=0, tiled=True)
    parts = jnp.split(out, [sum(widths[:k]) for k in range(1, len(widths))], axis=1)
    return tuple(
        (
            jnp.moveaxis(b.reshape(-1, *t.shape[1:]), 0, dim)
            for b, t, dim in zip(parts, turned, dims)
        )
    )


def cut_along(shard, dim, size):
    before, after = (shard.shape[:dim], shard.shape[dim + 1 :])
    return jnp.moveaxis(shard.reshape(*before, size, -1, *after), dim, 0)


def sent_and_summed(shard, axis, dim):
    size = lax.axis_size(axis)
    parts = lax.all_to_all(cut_along(shard, dim, size), axis, 0, 0, tiled=True)
    return jnp.sum(parts.astype(jnp.float32), axis=0)


def laid_out(parts, dim):
    shape = list(parts.shape[1:])
    shape[dim] *= parts.shape[0]
    return jnp.moveaxis(parts, 0, dim).reshape(shape)


def gathered_copies(shard, axis, dim):
    parts = from_everyone(shard, axis)
    return laid_out(parts, dim)


def pick_rows(restore_id, param_table):
    selector = (
        jnp.arange(param_table.shape[0], dtype=jnp.int32)[None, :] == restore_id[:, None]
    ).astype(jnp.float32)
    return jnp.dot(selector, param_table, precision=lax.Precision.HIGHEST)[0]


def norm_rows(values, gain_row):
    feature_count = values.shape[1] * lax.axis_size("row")
    totals = packed_total((jnp.sum(values, axis=1), jnp.sum(values * values, axis=1)), "row")
    average = totals[0][:, None] / feature_count
    spread = totals[1][:, None] / feature_count - average * average
    return ((values - average) * lax.rsqrt(spread + EPSILON) * gain_row).astype(jnp.bfloat16)


def move_halves(pieces, bit_total, device_index, exchange):
    for bit_number in range(bit_total):
        upper_side = device_index >> bit_number & 1 == 1
        outgoing = tuple(
            (jnp.where(upper_side, lower_part, upper_part) for lower_part, upper_part in pieces)
        )
        incoming = exchange(outgoing, bit_number)
        pieces = tuple(
            (
                (
                    jnp.where(upper_side, arrived, lower_part),
                    jnp.where(upper_side, upper_part, arrived),
                )
                for (lower_part, upper_part), arrived in zip(pieces, incoming)
            )
        )
    return pieces


def on_device(
    patches,
    embed_weight,
    embed_bias,
    old_in,
    old_out,
    restore_id,
    norm_gains,
    in_biases,
    out_biases,
    final_gain,
    check_weight,
):
    tiles_here, tile_rows, tile_cols = old_in.shape
    local_cols = tiles_here * tile_cols
    half_cols = local_cols // 2
    in_local = jnp.transpose(old_in, (1, 0, 2)).reshape(tile_rows, local_cols)
    out_local = old_out.reshape(local_cols, tile_rows)
    col_index = lax.axis_index("col")
    col_count = lax.axis_size("col")
    col_bits = col_count.bit_length() - 1
    share_rows = tile_rows // lax.axis_size("rep")
    first_row = lax.axis_index("rep") * share_rows
    in_share = lax.dynamic_slice_in_dim(in_local, first_row, share_rows, 0)
    out_share = lax.dynamic_slice_in_dim(out_local, first_row, share_rows, 1)
    pieces = (
        (in_share[:, :half_cols], in_share[:, half_cols:]),
        (out_share[:half_cols], out_share[half_cols:]),
    )
    pieces = move_halves(
        pieces,
        col_bits,
        col_index,
        lambda send_parts, bit_number: jax.tree.map(
            lambda part, own: part.astype(own.dtype),
            partner(for_sending(send_parts), "col", bit_number),
            send_parts,
        ),
    )
    gathered = rows_first(
        (pieces[0][0], pieces[0][1], pieces[1][0], pieces[1][1]), "rep", (0, 0, 1, 1)
    )
    in_weight = jnp.concatenate((gathered[0], gathered[1]), axis=0)
    out_weight = jnp.concatenate((gathered[2], gathered[3]), axis=1)
    layer_gain = pick_rows(restore_id, norm_gains)
    in_bias = pick_rows(restore_id, in_biases)
    out_bias = pick_rows(restore_id, out_biases)
    embedded = jnp.dot(patches, embed_weight, preferred_element_type=jnp.float32) + embed_bias
    normed = norm_rows(embedded, layer_gain)
    partial_pre = jnp.dot(
        lax.all_gather(normed, "col", axis=0, tiled=True),
        in_weight,
        preferred_element_type=jnp.float32,
    )
    pre_share = sent_and_summed(partial_pre.astype(jnp.bfloat16), "row", 0) + in_bias
    hidden = jax.nn.gelu(pre_share, approximate=False).astype(jnp.bfloat16)
    partial_branch = jnp.dot(
        gathered_copies(hidden, "row", 0), out_weight, preferred_element_type=jnp.float32
    )
    updated = embedded + sent_and_summed(partial_branch.astype(jnp.bfloat16), "col", 0) + out_bias
    final_normed = norm_rows(updated, final_gain)
    check_logits = lax.psum(
        jnp.dot(final_normed, check_weight, preferred_element_type=jnp.float32), "row"
    )
    return (in_weight, out_weight, check_logits)


def solution(mesh):
    placed = (
        P(("rep", "col"), None),
        P(None, "row"),
        P("row"),
        P(("row", "col"), None, None),
        P(("row", "col"), None, None),
        P(),
        P(None, "row"),
        P(None, "col"),
        P(None, "row"),
        P("row"),
        P("row", None),
    )
    return jax.shard_map(
        on_device,
        mesh=mesh,
        in_specs=placed,
        out_specs=(P("row", "col"), P("col", "row"), P(("rep", "col"), None)),
        check_vma=False,
    )
```

profile of v0, /device:TPU:6, one launch (start us, length us, event | category | flops | bytes accessed | tf_op | source)
XLA Modules:
  0.0 349.5 jit_solution(2980738248300091822)
XLA Ops:
  7.2 1.6 copy-done
  9.6 2.5 constant_dynamic-slice_fusion
  12.1 1.1 copy.25
  13.3 1.2 copy.26
  15.7 1.7 broadcast_select_fusion.12
  17.4 0.8 collective-permute-start.1
  18.2 1.7 broadcast_select_fusion.2
  20.0 1.2 collective-permute-start.5
  21.2 6.4 %collective-permute-done.1 = bf16[192,768]{1,0:T(8,128)(2,1)} collective-permute-done((bf16[192,768]{1,0:T(8,128)(2,1)}, bf16[192,768]{1,0:T(8,128)(2,1)}, u32[]{:S(2)}, u32[]{:S(2)}) %collective-permute-start.1) | collective-permute-done | bytes 294944 | tf_op jit(solution)/shard_map/ppermute | solution.py:35
  27.6 2.0 broadcast_select_fusion.15
  29.7 1.6 collective-permute-start.2
  31.3 2.7 collective-permute-done.5
  33.9 2.0 broadcast_select_fusion.5
  36.0 1.6 collective-permute-start.6
  37.6 4.3 %collective-permute-done.2 = bf16[192,768]{1,0:T(8,128)(2,1)} collective-permute-done((bf16[192,768]{1,0:T(8,128)(2,1)}, bf16[192,768]{1,0:T(8,128)(2,1)}, u32[]{:S(2)}, u32[]{:S(2)}) %collective-permute-start.2) | collective-permute-done | bytes 294944 | tf_op jit(solution)/shard_map/ppermute | solution.py:35
  41.9 1.1 broadcast_select_fusion.18
  43.1 4.2 %collective-permute-done.6 = bf16[768,192]{0,1:T(8,128)(2,1)} collective-permute-done((bf16[768,192]{0,1:T(8,128)(2,1)}, bf16[768,192]{0,1:T(8,128)(2,1)}, u32[]{:S(2)}, u32[]{:S(2)}) %collective-permute-start.6) | collective-permute-done | bytes 294944 | tf_op jit(solution)/shard_map/ppermute | solution.py:35
  47.2 1.1 broadcast_select_fusion.6
  48.6 1.5 collective-permute-done.3
  50.2 1.0 broadcast_select_fusion.17
  51.2 5.3 %collective-permute-done.7 = bf16[768,192]{0,1:T(8,128)(2,1)S(1)} collective-permute-done((bf16[768,192]{0,1:T(8,128)(2,1)S(1)}, bf16[768,192]{0,1:T(8,128)(2,1)S(1)}, u32[]{:S(2)}, u32[]{:S(2)}) %collective-permute-start.7) | collective-permute-done | bytes 294944 | tf_op jit(solution)/shard_map/ppermute | solution.py:35
  56.5 1.0 select_bitcast_fusion.1
  57.5 1.2 pad_maximum_fusion.2
  58.7 2.1 fusion.21
  61.5 6.1 %all-to-all-start = ((f32[4,1,128]{2,1,0:T(1,128)}), f32[4,1,128]{2,1,0:T(1,128)S(1)}, u32[]{:S(2)}, u32[]{:S(2)}) async-start(f32[4,1,128]{2,1,0:T(1,128)} %broadcast_in_dim.6), calls=%async_computation | async-start | bytes 4096 | tf_op jit(solution)/shard_map/all_to_all | solution.py:11
  68.5 6.7 %all-to-all-done = f32[4,1,128]{2,1,0:T(1,128)S(1)} async-done(((f32[4,1,128]{2,1,0:T(1,128)}), f32[4,1,128]{2,1,0:T(1,128)S(1)}, u32[]{:S(2)}, u32[]{:S(2)}) %all-to-all-start) | async-done | bytes 2080 | tf_op jit(solution)/shard_map/all_to_all | solution.py:11
  75.3 0.8 multiply_convert_fusion.1
  76.1 38.9 %all-gather.3.cloned.1.call-done = bf16[768,3072]{1,0:T(8,128)(2,1)} async-done(((bf16[192,3072]{1,0:T(8,128)(2,1)}), bf16[768,3072]{1,0:T(8,128)(2,1)}) %all-gather.3.cloned.1.call-update) | async-done | bytes 4718608 | tf_op jit(solution)/shard_map/all_gather | solution.py:42
  115.0 3.8 %slice_bitcast_fusion.1 = (bf16[768,768]{0,1:T(8,128)(2,1)S(1)}, bf16[768,768]{0,1:T(8,128)(2,1)}, bf16[768,768]{1,0:T(8,128)(2,1)S(1)}, bf16[768,768]{1,0:T(8,128)(2,1)S(1)}) fusion(bf16[768,3072]{1,0:T(8,128)(2,1)} %all-gather.3.cloned.1.call-done), kind=kLoop, calls=%fused_computation.9 | loop fusion | bytes 9437184 | tf_op jit(solution)/shard_map/transpose | solution.py:46
  118.8 1.6 pad_maximum_fusion
  120.3 34.0 %all-gather.5.cloned.1.call-done = bf16[1024,1536]{1,0:T(8,128)(2,1)} async-done(((bf16[64,1536]{1,0:T(8,128)(2,1)}), bf16[1024,1536]{1,0:T(8,128)(2,1)}) %all-gather.5.cloned.1.call-update) | async-done | bytes 3145744 | tf_op jit(solution)/shard_map/all_gather | solution.py:158
  154.3 6.4 %convolution_convert_fusion.1 = bf16[1024,768]{1,0:T(8,128)(2,1)} fusion(bf16[1024,1536]{1,0:T(8,128)(2,1)} %all-gather.5.cloned.1.call-done, bf16[1536,768]{1,0:T(8,128)(2,1)} %pad_maximum_fusion), kind=kOutput, calls=%fused_computation.6 | convolution fusion | flops 2416705536 | bytes 7077888 | tf_op jit(solution)/shard_map/dot_general | solution.py:157
  160.7 6.2 %all-to-all-start.1 = ((bf16[4,256,768]{2,1,0:T(8,128)(2,1)}), bf16[4,256,768]{2,1,0:T(8,128)(2,1)}, u32[]{:S(2)}, u32[]{:S(2)}) async-start(bf16[4,256,768]{2,1,0:T(8,128)(2,1)} %bitcast.54), calls=%async_computation.1 | async-start | bytes 3145728 | tf_op jit(solution)/shard_map/all_to_all | solution.py:59
  166.9 1.1 convolution_reduce_fusion.2
  168.0 28.4 %all-to-all-done.1 = bf16[4,256,768]{2,1,0:T(8,128)(2,1)} async-done(((bf16[4,256,768]{2,1,0:T(8,128)(2,1)}), bf16[4,256,768]{2,1,0:T(8,128)(2,1)}, u32[]{:S(2)}, u32[]{:S(2)}) %all-to-all-start.1) | async-done | bytes 1572896 | tf_op jit(solution)/shard_map/all_to_all | solution.py:59
  196.4 1.7 convert_reduce_fusion.1
  198.1 1.7 fusion.2
  199.9 50.6 %all_to_all.27 = bf16[4,256,768]{2,1,0:T(8,128)(2,1)S(1)} all-to-all(bf16[4,256,768]{2,1,0:T(8,128)(2,1)S(1)} %broadcast_in_dim.7), channel_id=1, replica_groups=mesh['rep'=4,'row'=4,'col'=16] {'row'}, dimensions={0} | all-to-all | bytes 3145728 | tf_op jit(solution)/shard_map/all_to_all | solution.py:11
  250.6 4.9 %convolution_convert_fusion = bf16[1024,1536]{1,0:T(8,128)(2,1)} fusion(bf16[1024,768]{1,0:T(8,128)(2,1)S(1)} %bitcast.55, bf16[768,768]{0,1:T(8,128)(2,1)S(1)} %copy-done.1, bf16[768,768]{0,1:T(8,128)(2,1)S(1)} %get-tuple-element.26), kind=kOutput, calls=%fused_computation.1 | convolution fusion | flops 2422210560 | bytes 7077888 | tf_op jit(solution)/shard_map/dot_general | solution.py:164
  255.5 6.5 %all-to-all-start.3 = ((bf16[16,64,1536]{2,1,0:T(8,128)(2,1)}), bf16[16,64,1536]{2,1,0:T(8,128)(2,1)}, u32[]{:S(2)}, u32[]{:S(2)}) async-start(bf16[16,64,1536]{2,1,0:T(8,128)(2,1)} %bitcast.53), calls=%async_computation.3 | async-start | bytes 6291456 | tf_op jit(solution)/shard_map/all_to_all | solution.py:59
  262.0 1.2 convolution_reduce_fusion
  263.2 43.8 %all-to-all-done.3 = bf16[16,64,1536]{2,1,0:T(8,128)(2,1)} async-done(((bf16[16,64,1536]{2,1,0:T(8,128)(2,1)}), bf16[16,64,1536]{2,1,0:T(8,128)(2,1)}, u32[]{:S(2)}, u32[]{:S(2)}) %all-to-all-start.3) | async-done | bytes 3145760 | tf_op jit(solution)/shard_map/all_to_all | solution.py:59
  307.0 2.4 convert_reduce_fusion
  309.4 0.9 fusion.20
  311.0 3.2 all-to-all-start.4
  314.2 2.8 pad_maximum_fusion.1
  317.1 4.3 %copy.23 = bf16[768,1536]{1,0:T(8,128)(2,1)} copy(bf16[768,1536]{0,1:T(8,128)(2,1)} %pad_maximum_fusion.1) | data formatting | bytes 4718592
  322.2 20.5 %psum.7 = f32[64,128]{1,0:T(8,128)} all-reduce(f32[64,128]{1,0:T(8,128)S(1)} %fusion.10), channel_id=1, replica_groups=mesh['rep'=4,'row'=4,'col'=16] {'row'}, use_global_device_ids=true, to_apply=%region_8.9 | all-reduce | flops 8192 | bytes 65536 | tf_op jit(solution)/shard_map/psum | solution.py:169
  (50 shorter events, 5.1 us)
Async XLA Ops:
  7.2 1.7 copy-start
  7.2 107.8 %all-gather.3.cloned.1.call-start = ((), (), s32[]{:S(2)}) async-start(), calls=%async_computation.5 | async-start | bytes 5898240 | tf_op jit(solution)/shard_map/all_gather | solution.py:42
  9.6 6.1 %collective-permute-start = (bf16[192,768]{1,0:T(8,128)(2,1)}, bf16[192,768]{1,0:T(8,128)(2,1)}, u32[]{:S(2)}, u32[]{:S(2)}) collective-permute-start(bf16[192,768]{1,0:T(8,128)(2,1)} %broadcast_select_fusion.9), channel_id=1, source_target_pairs={{0,1},{1,0},{2,3},{3,2},{4,5},{5,4},{6,7},{7,6},{8,9},{9,8},{10,11... | collective-permute-start | bytes 884744 | tf_op jit(solution)/shard_map/ppermute | solution.py:35
  15.2 3.1 collective-permute-start.4
  17.4 10.2 %collective-permute-start.1 = (bf16[192,768]{1,0:T(8,128)(2,1)}, bf16[192,768]{1,0:T(8,128)(2,1)}, u32[]{:S(2)}, u32[]{:S(2)}) collective-permute-start(bf16[192,768]{1,0:T(8,128)(2,1)} %broadcast_select_fusion.12), channel_id=1, source_target_pairs={{0,2},{1,3},{2,0},{3,1},{4,6},{5,7},{6,4},{7,5},{8,10},{9,11},{10,... | collective-permute-start | bytes 884744 | tf_op jit(solution)/shard_map/ppermute | solution.py:35
  20.0 14.0 %collective-permute-start.5 = (bf16[768,192]{0,1:T(8,128)(2,1)}, bf16[768,192]{0,1:T(8,128)(2,1)}, u32[]{:S(2)}, u32[]{:S(2)}) collective-permute-start(bf16[768,192]{0,1:T(8,128)(2,1)} %broadcast_select_fusion.2), channel_id=1, source_target_pairs={{0,2},{1,3},{2,0},{3,1},{4,6},{5,7},{6,4},{7,5},{8,10},{9,11},{10,... | collective-permute-start | bytes 884744 | tf_op jit(solution)/shard_map/ppermute | solution.py:35
  29.6 20.5 %copy-start.4 = (bf16[192,768]{1,0:T(8,128)(2,1)S(1)}, bf16[192,768]{1,0:T(8,128)(2,1)}, u32[]{:S(2)}) copy-start(bf16[192,768]{1,0:T(8,128)(2,1)} %get-tuple-element.21) | copy-start | bytes 884740
  29.6 20.5 %copy-start.5 = (bf16[192,768]{1,0:T(8,128)(2,1)S(1)}, bf16[192,768]{1,0:T(8,128)(2,1)}, u32[]{:S(2)}) copy-start(bf16[192,768]{1,0:T(8,128)(2,1)} %get-tuple-element.22) | copy-start | bytes 884740
  29.7 12.2 %collective-permute-start.2 = (bf16[192,768]{1,0:T(8,128)(2,1)}, bf16[192,768]{1,0:T(8,128)(2,1)}, u32[]{:S(2)}, u32[]{:S(2)}) collective-permute-start(bf16[192,768]{1,0:T(8,128)(2,1)} %get-tuple-element.20), channel_id=1, source_target_pairs={{0,4},{1,5},{2,6},{3,7},{4,0},{5,1},{6,2},{7,3},{8,12},{9,13},{10,... | collective-permute-start | bytes 884744 | tf_op jit(solution)/shard_map/ppermute | solution.py:35
  36.0 20.5 %copy-start.6 = (bf16[768,192]{0,1:T(8,128)(2,1)S(1)}, bf16[768,192]{0,1:T(8,128)(2,1)}, u32[]{:S(2)}) copy-start(bf16[768,192]{0,1:T(8,128)(2,1)} %get-tuple-element.24) | copy-start | bytes 884740
  36.0 20.5 %copy-start.7 = (bf16[768,192]{0,1:T(8,128)(2,1)S(1)}, bf16[768,192]{0,1:T(8,128)(2,1)}, u32[]{:S(2)}) copy-start(bf16[768,192]{0,1:T(8,128)(2,1)} %get-tuple-element.25) | copy-start | bytes 884740
  36.0 11.3 %collective-permute-start.6 = (bf16[768,192]{0,1:T(8,128)(2,1)}, bf16[768,192]{0,1:T(8,128)(2,1)}, u32[]{:S(2)}, u32[]{:S(2)}) collective-permute-start(bf16[768,192]{0,1:T(8,128)(2,1)} %get-tuple-element.23), channel_id=1, source_target_pairs={{0,4},{1,5},{2,6},{3,7},{4,0},{5,1},{6,2},{7,3},{8,12},{9,13},{10,... | collective-permute-start | bytes 884744 | tf_op jit(solution)/shard_map/ppermute | solution.py:35
  43.0 7.2 %collective-permute-start.3 = (bf16[192,768]{1,0:T(8,128)(2,1)S(1)}, bf16[192,768]{1,0:T(8,128)(2,1)S(1)}, u32[]{:S(2)}, u32[]{:S(2)}) collective-permute-start(bf16[192,768]{1,0:T(8,128)(2,1)S(1)} %broadcast_select_fusion.18), channel_id=1, source_target_pairs={{0,8},{1,9},{2,10},{3,11},{4,12},{5,13},{6,14},{7,15},{8,0},{9,1},... | collective-permute-start | bytes 884744 | tf_op jit(solution)/shard_map/ppermute | solution.py:35
  48.3 8.1 %collective-permute-start.7 = (bf16[768,192]{0,1:T(8,128)(2,1)S(1)}, bf16[768,192]{0,1:T(8,128)(2,1)S(1)}, u32[]{:S(2)}, u32[]{:S(2)}) collective-permute-start(bf16[768,192]{0,1:T(8,128)(2,1)S(1)} %broadcast_select_fusion.6), channel_id=1, source_target_pairs={{0,8},{1,9},{2,10},{3,11},{4,12},{5,13},{6,14},{7,15},{8,0},{9,1},... | collective-permute-start | bytes 884744 | tf_op jit(solution)/shard_map/ppermute | solution.py:35
  51.2 7.5 %copy-start.11 = (f32[1536]{0:T(1024)S(1)}, f32[1536]{0:T(1024)}, u32[]{:S(2)}) copy-start(f32[1536]{0:T(1024)} %param.13) | copy-start | bytes 18436
  57.5 10.7 %copy-start.10 = (f32[48,1536]{1,0:T(8,128)S(1)}, f32[48,1536]{1,0:T(8,128)}, u32[]{:S(2)}) copy-start(f32[48,1536]{1,0:T(8,128)} %param.17) | copy-start | bytes 884740
  60.8 15.3 %copy-start.2 = (f32[64,1536]{1,0:T(8,128)}, f32[64,1536]{1,0:T(8,128)S(1)}, u32[]{:S(2)}) copy-start(f32[64,1536]{1,0:T(8,128)S(1)} %get-tuple-element.40) | copy-start | bytes 1179652
  61.5 13.7 %all-to-all-start = ((f32[4,1,128]{2,1,0:T(1,128)}), f32[4,1,128]{2,1,0:T(1,128)S(1)}, u32[]{:S(2)}, u32[]{:S(2)}) async-start(f32[4,1,128]{2,1,0:T(1,128)} %broadcast_in_dim.6), calls=%async_computation | async-start | bytes 4096 | tf_op jit(solution)/shard_map/all_to_all | solution.py:11
  67.6 86.7 %all-gather.5.cloned.1.call-start = ((), (), s32[]{:S(2)}) async-start(), calls=%async_computation.6 | async-start | bytes 3342336 | tf_op jit(solution)/shard_map/all_gather | solution.py:158
  160.7 35.7 %all-to-all-start.1 = ((bf16[4,256,768]{2,1,0:T(8,128)(2,1)}), bf16[4,256,768]{2,1,0:T(8,128)(2,1)}, u32[]{:S(2)}, u32[]{:S(2)}) async-start(bf16[4,256,768]{2,1,0:T(8,128)(2,1)} %bitcast.54), calls=%async_computation.1 | async-start | bytes 3145728 | tf_op jit(solution)/shard_map/all_to_all | solution.py:59
  199.8 50.8 %copy-start.1 = (bf16[768,768]{0,1:T(8,128)(2,1)S(1)}, bf16[768,768]{0,1:T(8,128)(2,1)}, u32[]{:S(2)}) copy-start(bf16[768,768]{0,1:T(8,128)(2,1)} %get-tuple-element.27) | copy-start | bytes 3538948
  255.5 51.5 %all-to-all-start.3 = ((bf16[16,64,1536]{2,1,0:T(8,128)(2,1)}), bf16[16,64,1536]{2,1,0:T(8,128)(2,1)}, u32[]{:S(2)}, u32[]{:S(2)}) async-start(bf16[16,64,1536]{2,1,0:T(8,128)(2,1)} %bitcast.53), calls=%async_computation.3 | async-start | bytes 6291456 | tf_op jit(solution)/shard_map/all_to_all | solution.py:59
  307.0 2.4 copy-start.3
  311.0 10.8 %all-to-all-start.4 = ((f32[4,1,128]{2,1,0:T(1,128)}), f32[4,1,128]{2,1,0:T(1,128)S(1)}, u32[]{:S(2)}, u32[]{:S(2)}) async-start(f32[4,1,128]{2,1,0:T(1,128)} %broadcast_in_dim.8), calls=%async_computation.4 | async-start | bytes 4096 | tf_op jit(solution)/shard_map/all_to_all | solution.py:11
  317.1 4.8 %copy-start.8 = (f32[64,1536]{1,0:T(8,128)S(1)}, f32[64,1536]{1,0:T(8,128)}, u32[]{:S(2)}) copy-start(f32[64,1536]{1,0:T(8,128)} %get-tuple-element.19) | copy-start | bytes 1179652
  317.1 4.8 %copy-start.9 = (bf16[1536,128]{1,0:T(8,128)(2,1)S(1)}, bf16[1536,128]{1,0:T(8,128)(2,1)}, u32[]{:S(2)}) copy-start(bf16[1536,128]{1,0:T(8,128)(2,1)} %param.21) | copy-start | bytes 1179652
  317.1 4.8 %copy-start.12 = (f32[1536]{0:T(1024)S(1)}, f32[1536]{0:T(1024)}, u32[]{:S(2)}) copy-start(f32[1536]{0:T(1024)} %param.20) | copy-start | bytes 18436
Sparse Core Ops, SparseCore 0:
  58.8 56.1 all-gather.2
  116.8 37.4 all-gather.4
where the time goes:
time: 351 us; the launch traced here: 350 us
  waiting for transfers between devices  177 us (50%)
  blocking collectives  71.1 us (20%)
  starting transfers between devices  28.2 us (8%)
  other arithmetic  26.7 us (8%)
  matrix products  16.2 us (5%)
  local copies, waits for them, and re-layouts  15.9 us (5%)
  between operations  14.9 us (4%)
    all_to_all x2, waiting for transfers between devices, sent_and_summed(): parts = lax.all_to_all(cut_along(shard, dim, size), axis, 0, 0, tiled=True)  72.2 us
    all_to_all x1, blocking collectives, from_everyone(): lax.all_to_all(jnp.broadcast_to(shard[None], (size, *shard.shape)), axis,...  50.6 us
    all_gather x1, waiting for transfers between devices, rows_first(): out = lax.all_gather(both, axis, axis=0, tiled=True)  38.9 us
    all_gather x1, waiting for transfers between devices, on_device(): lax.all_gather(normed, 'col', axis=0, tiled=True)  34 us
    ppermute x8, waiting for transfers between devices, partner(): return lax.ppermute(value, axis, pairs)  24.3 us
    psum x1, blocking collectives, on_device(): lax.psum(jnp.dot(final_normed, check_weight, preferred_element_type=jnp.f...  20.5 us
    all_to_all x2, starting transfers between devices, sent_and_summed(): parts = lax.all_to_all(cut_along(shard, dim, size), axis, 0, 0, tiled=True)  12.7 us
    select_n x8, other arithmetic, move_halves(): jnp.where(upper_side, lower_part, upper_part)  11.2 us
  transfers between devices with their start and end apart: 14, of which 12 were waited for; matrix products, arithmetic and copies ran while one was open for 10% of the time, Pallas kernels for 0%

commit v1 on v0

--- a/solution.py
+++ b/solution.py
@@ -4,6 +4,13 @@
 from jax.sharding import PartitionSpec as P
 
 EPSILON = 1e-06
+
+
+def exchange_gather(x, mesh_axis, dim):
+    devices = lax.axis_size(mesh_axis)
+    parts = jnp.stack([x for _ in range(devices)])
+    parts = lax.all_to_all(parts, mesh_axis, split_axis=0, concat_axis=0)
+    return jnp.concatenate(parts, axis=dim)
 
 
 def from_everyone(shard, axis):
@@ -155,9 +162,7 @@
     embedded = jnp.dot(patches, embed_weight, preferred_element_type=jnp.float32) + embed_bias
     normed = norm_rows(embedded, layer_gain)
     partial_pre = jnp.dot(
-        lax.all_gather(normed, "col", axis=0, tiled=True),
-        in_weight,
-        preferred_element_type=jnp.float32,
+        exchange_gather(normed, "col", 0), in_weight, preferred_element_type=jnp.float32
     )
     pre_share = sent_and_summed(partial_pre.astype(jnp.bfloat16), "row", 0) + in_bias
     hidden = jax.nn.gelu(pre_share, approximate=False).astype(jnp.bfloat16)

time: 351 us -> 325 us (0.926)
  waiting for transfers between devices: 177 us -> 154 us
  blocking collectives: 71.1 us -> 56.5 us
  starting transfers between devices: 28.2 us -> 37.9 us
    all_gather x1 -> x0, waiting for transfers between devices: 34 us -> none  [on_device(): lax.all_gather(normed, 'col', axis=0, tiled=True)]
    all_to_all x1, blocking collectives: 50.6 us -> 36 us  [from_everyone(): lax.all_to_all(jnp.broadcast_to(shard[None], (size, *shard.shape)), axis,...]
    all_to_all x2, waiting for transfers between devices: 72.2 us -> 83.1 us  [sent_and_summed(): parts = lax.all_to_all(cut_along(shard, dim, size), axis, 0, 0, tiled=True)]
    all_to_all x0 -> x1, waiting for transfers between devices: none -> 9.99 us  [exchange_gather(): parts = lax.all_to_all(parts, mesh_axis, split_axis=0, concat_axis=0)]
    all_gather x1, waiting for transfers between devices: 38.9 us -> 29.8 us  [rows_first(): out = lax.all_gather(both, axis, axis=0, tiled=True)]
    all_to_all x0 -> x1, starting transfers between devices: none -> 7.74 us  [exchange_gather(): parts = lax.all_to_all(parts, mesh_axis, split_axis=0, concat_axis=0)]
  transfers between devices with their start and end apart: 14 -> 14, of which waited for: 12 -> 12; matrix products, arithmetic and copies ran while one was open for 10% -> 11% of each run, Pallas kernels for 0% -> 0%
where the time goes in v1:
time: 325 us; the launch traced here: 324 us
  waiting for transfers between devices  154 us (47%)
  blocking collectives  56.5 us (17%)
  starting transfers between devices  37.9 us (12%)
  other arithmetic  26 us (8%)
  local copies, waits for them, and re-layouts  17.9 us (6%)
  matrix products  16.1 us (5%)
  between operations  14.9 us (5%)
    all_to_all x2, waiting for transfers between devices, sent_and_summed(): parts = lax.all_to_all(cut_along(shard, dim, size), axis, 0, 0, tiled=True)  83.1 us
    all_to_all x1, blocking collectives, from_everyone(): lax.all_to_all(jnp.broadcast_to(shard[None], (size, *shard.shape)), axis,...  36 us
    all_gather x1, waiting for transfers between devices, rows_first(): out = lax.all_gather(both, axis, axis=0, tiled=True)  29.8 us
    ppermute x8, waiting for transfers between devices, partner(): return lax.ppermute(value, axis, pairs)  24.3 us
    psum x1, blocking collectives, on_device(): lax.psum(jnp.dot(final_normed, check_weight, preferred_element_type=jnp.f...  20.5 us
    all_to_all x2, starting transfers between devices, sent_and_summed(): parts = lax.all_to_all(cut_along(shard, dim, size), axis, 0, 0, tiled=True)  14.7 us
    select_n x8, other arithmetic, move_halves(): jnp.where(upper_side, lower_part, upper_part)  11.2 us
    all_to_all x1, waiting for transfers between devices, exchange_gather(): parts = lax.all_to_all(parts, mesh_axis, split_axis=0, concat_axis=0)  9.99 us
  transfers between devices with their start and end apart: 14, of which 12 were waited for; matrix products, arithmetic and copies ran while one was open for 11% of the time, Pallas kernels for 0%

profile of v1, /device:TPU:6, one launch (start us, length us, event | category | flops | bytes accessed | tf_op | source)
XLA Modules:
  0.0 323.7 jit_solution(3509081405633972241)
XLA Ops:
  7.2 1.6 copy-done
  9.6 2.5 constant_dynamic-slice_fusion
  12.1 1.1 copy.25
  13.3 1.2 copy.26
  15.7 1.7 broadcast_select_fusion.12
  18.2 1.7 broadcast_select_fusion.2
  20.0 1.2 collective-permute-start.5
  21.2 6.4 %collective-permute-done.1 = bf16[192,768]{1,0:T(8,128)(2,1)} collective-permute-done((bf16[192,768]{1,0:T(8,128)(2,1)}, bf16[192,768]{1,0:T(8,128)(2,1)}, u32[]{:S(2)}, u32[]{:S(2)}) %collective-permute-start.1) | collective-permute-done | bytes 294944 | tf_op jit(solution)/shard_map/ppermute | solution.py:42
  27.6 2.0 broadcast_select_fusion.15
  29.7 1.6 collective-permute-start.2
  31.3 2.6 collective-permute-done.5
  33.9 2.0 broadcast_select_fusion.5
  36.0 1.6 collective-permute-start.6
  37.6 4.3 %collective-permute-done.2 = bf16[192,768]{1,0:T(8,128)(2,1)} collective-permute-done((bf16[192,768]{1,0:T(8,128)(2,1)}, bf16[192,768]{1,0:T(8,128)(2,1)}, u32[]{:S(2)}, u32[]{:S(2)}) %collective-permute-start.2) | collective-permute-done | bytes 294944 | tf_op jit(solution)/shard_map/ppermute | solution.py:42
  41.9 1.1 broadcast_select_fusion.18
  43.1 4.2 %collective-permute-done.6 = bf16[768,192]{0,1:T(8,128)(2,1)} collective-permute-done((bf16[768,192]{0,1:T(8,128)(2,1)}, bf16[768,192]{0,1:T(8,128)(2,1)}, u32[]{:S(2)}, u32[]{:S(2)}) %collective-permute-start.6) | collective-permute-done | bytes 294944 | tf_op jit(solution)/shard_map/ppermute | solution.py:42
  47.2 1.1 broadcast_select_fusion.6
  48.6 1.5 collective-permute-done.3
  50.2 1.0 broadcast_select_fusion.17
  51.2 5.3 %collective-permute-done.7 = bf16[768,192]{0,1:T(8,128)(2,1)S(1)} collective-permute-done((bf16[768,192]{0,1:T(8,128)(2,1)S(1)}, bf16[768,192]{0,1:T(8,128)(2,1)S(1)}, u32[]{:S(2)}, u32[]{:S(2)}) %collective-permute-start.7) | collective-permute-done | bytes 294944 | tf_op jit(solution)/shard_map/ppermute | solution.py:42
  56.5 1.0 select_bitcast_fusion.1
  57.5 1.2 pad_maximum_fusion.2
  58.7 2.1 fusion.21
  61.5 6.1 %all-to-all-start = ((f32[4,1,128]{2,1,0:T(1,128)}), f32[4,1,128]{2,1,0:T(1,128)S(1)}, u32[]{:S(2)}, u32[]{:S(2)}) async-start(f32[4,1,128]{2,1,0:T(1,128)} %broadcast_in_dim.6), calls=%async_computation | async-start | bytes 4096 | tf_op jit(solution)/shard_map/all_to_all | solution.py:18
  68.5 6.7 %all-to-all-done = f32[4,1,128]{2,1,0:T(1,128)S(1)} async-done(((f32[4,1,128]{2,1,0:T(1,128)}), f32[4,1,128]{2,1,0:T(1,128)S(1)}, u32[]{:S(2)}, u32[]{:S(2)}) %all-to-all-start) | async-done | bytes 2080 | tf_op jit(solution)/shard_map/all_to_all | solution.py:18
  75.4 2.1 stack.2
  77.5 7.7 %all-to-all-start.1 = ((bf16[16,64,1536]{2,1,0:T(8,128)(2,1)}), bf16[16,64,1536]{2,1,0:T(8,128)(2,1)}, u32[]{:S(2)}, u32[]{:S(2)}) async-start(bf16[16,64,1536]{2,1,0:T(8,128)(2,1)} %stack.2), calls=%async_computation.1 | async-start | bytes 6291456 | tf_op jit(solution)/shard_map/all_to_all | solution.py:12
  85.2 29.8 %all-gather.2.cloned.1.call-done = bf16[768,3072]{1,0:T(8,128)(2,1)} async-done(((bf16[192,3072]{1,0:T(8,128)(2,1)}), bf16[768,3072]{1,0:T(8,128)(2,1)}) %all-gather.2.cloned.1.call-update) | async-done | bytes 4718608 | tf_op jit(solution)/shard_map/all_gather | solution.py:49
  115.0 3.7 %slice_bitcast_fusion.1 = (bf16[768,768]{0,1:T(8,128)(2,1)S(1)}, bf16[768,768]{0,1:T(8,128)(2,1)}, bf16[768,768]{1,0:T(8,128)(2,1)S(1)}, bf16[768,768]{1,0:T(8,128)(2,1)S(1)}) fusion(bf16[768,3072]{1,0:T(8,128)(2,1)} %all-gather.2.cloned.1.call-done), kind=kLoop, calls=%fused_computation.9 | loop fusion | bytes 9437184 | tf_op jit(solution)/shard_map/transpose | solution.py:53
  118.7 1.6 pad_maximum_fusion
  120.2 10.0 %all-to-all-done.1 = bf16[16,64,1536]{2,1,0:T(8,128)(2,1)} async-done(((bf16[16,64,1536]{2,1,0:T(8,128)(2,1)}), bf16[16,64,1536]{2,1,0:T(8,128)(2,1)}, u32[]{:S(2)}, u32[]{:S(2)}) %all-to-all-start.1) | async-done | bytes 3145760 | tf_op jit(solution)/shard_map/all_to_all | solution.py:12
  130.2 6.4 %convolution_convert_fusion.1 = bf16[1024,768]{1,0:T(8,128)(2,1)} fusion(bf16[1024,1536]{1,0:T(8,128)(2,1)} %bitcast.10, bf16[1536,768]{1,0:T(8,128)(2,1)} %pad_maximum_fusion), kind=kOutput, calls=%fused_computation.6 | convolution fusion | flops 2416705536 | bytes 7077888 | tf_op jit(solution)/shard_map/dot_general | solution.py:164
  136.6 4.5 %all-to-all-start.2 = ((bf16[4,256,768]{2,1,0:T(8,128)(2,1)}), bf16[4,256,768]{2,1,0:T(8,128)(2,1)}, u32[]{:S(2)}, u32[]{:S(2)}) async-start(bf16[4,256,768]{2,1,0:T(8,128)(2,1)} %bitcast.55), calls=%async_computation.2 | async-start | bytes 3145728 | tf_op jit(solution)/shard_map/all_to_all | solution.py:66
  141.1 1.1 convolution_reduce_fusion.2
  142.2 39.3 %all-to-all-done.2 = bf16[4,256,768]{2,1,0:T(8,128)(2,1)} async-done(((bf16[4,256,768]{2,1,0:T(8,128)(2,1)}), bf16[4,256,768]{2,1,0:T(8,128)(2,1)}, u32[]{:S(2)}, u32[]{:S(2)}) %all-to-all-start.2) | async-done | bytes 1572896 | tf_op jit(solution)/shard_map/all_to_all | solution.py:66
  181.6 1.7 convert_reduce_fusion.1
  183.3 1.7 fusion.2
  185.1 36.0 %all_to_all.32 = bf16[4,256,768]{2,1,0:T(8,128)(2,1)S(1)} all-to-all(bf16[4,256,768]{2,1,0:T(8,128)(2,1)S(1)} %broadcast_in_dim.7), channel_id=1, replica_groups=mesh['rep'=4,'row'=4,'col'=16] {'row'}, dimensions={0} | all-to-all | bytes 3145728 | tf_op jit(solution)/shard_map/all_to_all | solution.py:18
  221.1 4.9 %convolution_convert_fusion = bf16[1024,1536]{1,0:T(8,128)(2,1)} fusion(bf16[1024,768]{1,0:T(8,128)(2,1)S(1)} %bitcast.56, bf16[768,768]{0,1:T(8,128)(2,1)S(1)} %copy-done.1, bf16[768,768]{0,1:T(8,128)(2,1)S(1)} %get-tuple-element.26), kind=kOutput, calls=%fused_computation.1 | convolution fusion | flops 2422210560 | bytes 7077888 | tf_op jit(solution)/shard_map/dot_general | solution.py:169
  226.0 10.2 %all-to-all-start.4 = ((bf16[16,64,1536]{2,1,0:T(8,128)(2,1)}), bf16[16,64,1536]{2,1,0:T(8,128)(2,1)}, u32[]{:S(2)}, u32[]{:S(2)}) async-start(bf16[16,64,1536]{2,1,0:T(8,128)(2,1)} %bitcast.54), calls=%async_computation.4 | async-start | bytes 6291456 | tf_op jit(solution)/shard_map/all_to_all | solution.py:66
  236.2 1.2 convolution_reduce_fusion
  237.4 43.8 %all-to-all-done.4 = bf16[16,64,1536]{2,1,0:T(8,128)(2,1)} async-done(((bf16[16,64,1536]{2,1,0:T(8,128)(2,1)}), bf16[16,64,1536]{2,1,0:T(8,128)(2,1)}, u32[]{:S(2)}, u32[]{:S(2)}) %all-to-all-start.4) | async-done | bytes 3145760 | tf_op jit(solution)/shard_map/all_to_all | solution.py:66
  281.2 2.4 convert_reduce_fusion
  283.6 0.9 fusion.20
  285.2 3.2 all-to-all-start.5
  288.4 2.8 pad_maximum_fusion.1
  291.3 4.3 %copy.23 = bf16[768,1536]{1,0:T(8,128)(2,1)} copy(bf16[768,1536]{0,1:T(8,128)(2,1)} %pad_maximum_fusion.1) | data formatting | bytes 4718592
  296.4 20.5 %psum.7 = f32[64,128]{1,0:T(8,128)} all-reduce(f32[64,128]{1,0:T(8,128)S(1)} %fusion.10), channel_id=1, replica_groups=mesh['rep'=4,'row'=4,'col'=16] {'row'}, use_global_device_ids=true, to_apply=%region_8.9 | all-reduce | flops 8192 | bytes 65536 | tf_op jit(solution)/shard_map/psum | solution.py:174
  (50 shorter events, 6.1 us)
Async XLA Ops:
  7.2 1.7 copy-start
  7.2 107.8 %all-gather.2.cloned.1.call-start = ((), (), s32[]{:S(2)}) async-start(), calls=%async_computation.6 | async-start | bytes 5898240 | tf_op jit(solution)/shard_map/all_gather | solution.py:49
  9.6 6.1 %collective-permute-start = (bf16[192,768]{1,0:T(8,128)(2,1)}, bf16[192,768]{1,0:T(8,128)(2,1)}, u32[]{:S(2)}, u32[]{:S(2)}) collective-permute-start(bf16[192,768]{1,0:T(8,128)(2,1)} %broadcast_select_fusion.9), channel_id=1, source_target_pairs={{0,1},{1,0},{2,3},{3,2},{4,5},{5,4},{6,7},{7,6},{8,9},{9,8},{10,11... | collective-permute-start | bytes 884744 | tf_op jit(solution)/shard_map/ppermute | solution.py:42
  15.2 3.1 collective-permute-start.4
  17.4 10.2 %collective-permute-start.1 = (bf16[192,768]{1,0:T(8,128)(2,1)}, bf16[192,768]{1,0:T(8,128)(2,1)}, u32[]{:S(2)}, u32[]{:S(2)}) collective-permute-start(bf16[192,768]{1,0:T(8,128)(2,1)} %broadcast_select_fusion.12), channel_id=1, source_target_pairs={{0,2},{1,3},{2,0},{3,1},{4,6},{5,7},{6,4},{7,5},{8,10},{9,11},{10,... | collective-permute-start | bytes 884744 | tf_op jit(solution)/shard_map/ppermute | solution.py:42
  20.0 14.0 %collective-permute-start.5 = (bf16[768,192]{0,1:T(8,128)(2,1)}, bf16[768,192]{0,1:T(8,128)(2,1)}, u32[]{:S(2)}, u32[]{:S(2)}) collective-permute-start(bf16[768,192]{0,1:T(8,128)(2,1)} %broadcast_select_fusion.2), channel_id=1, source_target_pairs={{0,2},{1,3},{2,0},{3,1},{4,6},{5,7},{6,4},{7,5},{8,10},{9,11},{10,... | collective-permute-start | bytes 884744 | tf_op jit(solution)/shard_map/ppermute | solution.py:42
  29.7 20.5 %copy-start.4 = (bf16[192,768]{1,0:T(8,128)(2,1)S(1)}, bf16[192,768]{1,0:T(8,128)(2,1)}, u32[]{:S(2)}) copy-start(bf16[192,768]{1,0:T(8,128)(2,1)} %get-tuple-element.21) | copy-start | bytes 884740
  29.7 20.5 %copy-start.5 = (bf16[192,768]{1,0:T(8,128)(2,1)S(1)}, bf16[192,768]{1,0:T(8,128)(2,1)}, u32[]{:S(2)}) copy-start(bf16[192,768]{1,0:T(8,128)(2,1)} %get-tuple-element.22) | copy-start | bytes 884740
  29.7 12.2 %collective-permute-start.2 = (bf16[192,768]{1,0:T(8,128)(2,1)}, bf16[192,768]{1,0:T(8,128)(2,1)}, u32[]{:S(2)}, u32[]{:S(2)}) collective-permute-start(bf16[192,768]{1,0:T(8,128)(2,1)} %get-tuple-element.20), channel_id=1, source_target_pairs={{0,4},{1,5},{2,6},{3,7},{4,0},{5,1},{6,2},{7,3},{8,12},{9,13},{10,... | collective-permute-start | bytes 884744 | tf_op jit(solution)/shard_map/ppermute | solution.py:42
  36.0 20.5 %copy-start.6 = (bf16[768,192]{0,1:T(8,128)(2,1)S(1)}, bf16[768,192]{0,1:T(8,128)(2,1)}, u32[]{:S(2)}) copy-start(bf16[768,192]{0,1:T(8,128)(2,1)} %get-tuple-element.24) | copy-start | bytes 884740
  36.0 20.5 %copy-start.7 = (bf16[768,192]{0,1:T(8,128)(2,1)S(1)}, bf16[768,192]{0,1:T(8,128)(2,1)}, u32[]{:S(2)}) copy-start(bf16[768,192]{0,1:T(8,128)(2,1)} %get-tuple-element.25) | copy-start | bytes 884740
  36.0 11.3 %collective-permute-start.6 = (bf16[768,192]{0,1:T(8,128)(2,1)}, bf16[768,192]{0,1:T(8,128)(2,1)}, u32[]{:S(2)}, u32[]{:S(2)}) collective-permute-start(bf16[768,192]{0,1:T(8,128)(2,1)} %get-tuple-element.23), channel_id=1, source_target_pairs={{0,4},{1,5},{2,6},{3,7},{4,0},{5,1},{6,2},{7,3},{8,12},{9,13},{10,... | collective-permute-start | bytes 884744 | tf_op jit(solution)/shard_map/ppermute | solution.py:42
  43.0 7.2 %collective-permute-start.3 = (bf16[192,768]{1,0:T(8,128)(2,1)S(1)}, bf16[192,768]{1,0:T(8,128)(2,1)S(1)}, u32[]{:S(2)}, u32[]{:S(2)}) collective-permute-start(bf16[192,768]{1,0:T(8,128)(2,1)S(1)} %broadcast_select_fusion.18), channel_id=1, source_target_pairs={{0,8},{1,9},{2,10},{3,11},{4,12},{5,13},{6,14},{7,15},{8,0},{9,1},... | collective-permute-start | bytes 884744 | tf_op jit(solution)/shard_map/ppermute | solution.py:42
  48.3 8.1 %collective-permute-start.7 = (bf16[768,192]{0,1:T(8,128)(2,1)S(1)}, bf16[768,192]{0,1:T(8,128)(2,1)S(1)}, u32[]{:S(2)}, u32[]{:S(2)}) collective-permute-start(bf16[768,192]{0,1:T(8,128)(2,1)S(1)} %broadcast_select_fusion.6), channel_id=1, source_target_pairs={{0,8},{1,9},{2,10},{3,11},{4,12},{5,13},{6,14},{7,15},{8,0},{9,1},... | collective-permute-start | bytes 884744 | tf_op jit(solution)/shard_map/ppermute | solution.py:42
  51.2 7.5 %copy-start.11 = (f32[1536]{0:T(1024)S(1)}, f32[1536]{0:T(1024)}, u32[]{:S(2)}) copy-start(f32[1536]{0:T(1024)} %param.13) | copy-start | bytes 18436
  57.5 10.7 %copy-start.10 = (f32[48,1536]{1,0:T(8,128)S(1)}, f32[48,1536]{1,0:T(8,128)}, u32[]{:S(2)}) copy-start(f32[48,1536]{1,0:T(8,128)} %param.17) | copy-start | bytes 884740
  60.8 16.7 %copy-start.2 = (f32[64,1536]{1,0:T(8,128)}, f32[64,1536]{1,0:T(8,128)S(1)}, u32[]{:S(2)}) copy-start(f32[64,1536]{1,0:T(8,128)S(1)} %get-tuple-element.40) | copy-start | bytes 1179652
  61.5 13.7 %all-to-all-start = ((f32[4,1,128]{2,1,0:T(1,128)}), f32[4,1,128]{2,1,0:T(1,128)S(1)}, u32[]{:S(2)}, u32[]{:S(2)}) async-start(f32[4,1,128]{2,1,0:T(1,128)} %broadcast_in_dim.6), calls=%async_computation | async-start | bytes 4096 | tf_op jit(solution)/shard_map/all_to_all | solution.py:18
  77.5 52.7 %all-to-all-start.1 = ((bf16[16,64,1536]{2,1,0:T(8,128)(2,1)}), bf16[16,64,1536]{2,1,0:T(8,128)(2,1)}, u32[]{:S(2)}, u32[]{:S(2)}) async-start(bf16[16,64,1536]{2,1,0:T(8,128)(2,1)} %stack.2), calls=%async_computation.1 | async-start | bytes 6291456 | tf_op jit(solution)/shard_map/all_to_all | solution.py:12
  136.6 45.0 %all-to-all-start.2 = ((bf16[4,256,768]{2,1,0:T(8,128)(2,1)}), bf16[4,256,768]{2,1,0:T(8,128)(2,1)}, u32[]{:S(2)}, u32[]{:S(2)}) async-start(bf16[4,256,768]{2,1,0:T(8,128)(2,1)} %bitcast.55), calls=%async_computation.2 | async-start | bytes 3145728 | tf_op jit(solution)/shard_map/all_to_all | solution.py:66
  185.0 36.1 %copy-start.1 = (bf16[768,768]{0,1:T(8,128)(2,1)S(1)}, bf16[768,768]{0,1:T(8,128)(2,1)}, u32[]{:S(2)}) copy-start(bf16[768,768]{0,1:T(8,128)(2,1)} %get-tuple-element.27) | copy-start | bytes 3538948
  226.0 55.1 %all-to-all-start.4 = ((bf16[16,64,1536]{2,1,0:T(8,128)(2,1)}), bf16[16,64,1536]{2,1,0:T(8,128)(2,1)}, u32[]{:S(2)}, u32[]{:S(2)}) async-start(bf16[16,64,1536]{2,1,0:T(8,128)(2,1)} %bitcast.54), calls=%async_computation.4 | async-start | bytes 6291456 | tf_op jit(solution)/shard_map/all_to_all | solution.py:66
  281.2 2.4 copy-start.3
  285.2 10.8 %all-to-all-start.5 = ((f32[4,1,128]{2,1,0:T(1,128)}), f32[4,1,128]{2,1,0:T(1,128)S(1)}, u32[]{:S(2)}, u32[]{:S(2)}) async-start(f32[4,1,128]{2,1,0:T(1,128)} %broadcast_in_dim.8), calls=%async_computation.5 | async-start | bytes 4096 | tf_op jit(solution)/shard_map/all_to_all | solution.py:18
  291.3 4.8 %copy-start.8 = (f32[64,1536]{1,0:T(8,128)S(1)}, f32[64,1536]{1,0:T(8,128)}, u32[]{:S(2)}) copy-start(f32[64,1536]{1,0:T(8,128)} %get-tuple-element.19) | copy-start | bytes 1179652
  291.3 4.8 %copy-start.9 = (bf16[1536,128]{1,0:T(8,128)(2,1)S(1)}, bf16[1536,128]{1,0:T(8,128)(2,1)}, u32[]{:S(2)}) copy-start(bf16[1536,128]{1,0:T(8,128)(2,1)} %param.21) | copy-start | bytes 1179652
  291.3 4.8 %copy-start.12 = (f32[1536]{0:T(1024)S(1)}, f32[1536]{0:T(1024)}, u32[]{:S(2)}) copy-start(f32[1536]{0:T(1024)} %param.20) | copy-start | bytes 18436
Sparse Core Ops, SparseCore 0:
  58.8 56.1 all-gather.1
